TPU v7x, 512 devices: a whole 4x4x16 slice. The times are simulated.
512 devices in a mesh: row: 32 (over z, core), col: 16 (over x, y).
Axes of the slice: x: 4, y: 4, z: 16, core: 2. Of those that a mesh axis runs over, the one named last changes fastest.
Arguments:
- factor: bfloat16 [8192, 8192], P('row', 'col'), as said below
- sel_tiles: int32 [32], replicated, may hold values from 0 to 63, as said below
- coupling: bfloat16 [8192, 2048], P('col', 'row')
Outputs:
- root_inverse: float32 [8192, 8192], P('row', 'col')
- child_inverse: float32 [2048, 8192], P('col', 'row')
Inputs may be any that keep to these rules, and one draw needn't show every extreme that they name: sel_tiles holds 32 distinct tile indices in increasing order; rows of coupling outside the listed tiles are zero. factor is lower triangular with a diagonal between 1 and 1.5.
All inputs are finite; a program needn't handle non-finite values.
Results may differ from a plain program's by a relative error of at most 0.003.
Values may be sent and summed in bfloat16 or wider, within the bound.
A program may use at most 64 MiB of HBM per device.

v0:
```python
import jax
import jax.numpy as jnp
from jax import lax
from jax.sharding import PartitionSpec as P

TILE = 128


def from_root(value, axis, source):
    kept = jnp.where(lax.axis_index(axis) == source, value, 0).astype(value.dtype)
    return lax.psum(kept, axis)


def in_blocks(value, dim, devices):
    lengths = value.shape
    parts = value.reshape(*lengths[:dim], devices, lengths[dim] // devices, *lengths[dim + 1 :])
    return jnp.moveaxis(parts, dim, 0)


def summed_on_arrival(value, axis, dim):
    devices = lax.axis_size(axis)
    parts = lax.all_to_all(in_blocks(value, dim, devices), axis, 0, 0, tiled=True)
    return jnp.sum(parts, axis=0)


def body(factor, sel_tiles, coupling):
    rows_here = factor.shape[0]
    row_index = lax.axis_index("row")
    whole = lax.all_gather(factor, "row", axis=0, tiled=True)
    ratio = lax.axis_size("row") // lax.axis_size("col")
    offset = row_index % ratio * rows_here
    piece = lax.dynamic_slice_in_dim(whole, offset, rows_here, 1)
    partner = from_root(piece, "col", row_index // ratio)
    gram = lax.dot_general(
        partner, whole, (((0,), (0,)), ((), ())), preferred_element_type=jnp.float32
    )
    coupling_full = lax.all_gather(coupling, "row", axis=1, tiled=True)
    rounded = gram.astype(jnp.bfloat16)
    global_rows = row_index * rows_here + jnp.arange(rows_here, dtype=jnp.int32)
    member = jnp.any((global_rows // TILE)[:, None] == sel_tiles[None, :], axis=1)
    summed = summed_on_arrival(
        lax.dot_general(
            coupling_full, rounded, (((0,), (1,)), ((), ())), preferred_element_type=jnp.float32
        ),
        "col",
        0,
    )
    child = jnp.where(member[None, :], -summed, jnp.float32(0.0))
    return (gram, child)


def solution(mesh):
    placed = (P("row", "col"), P(), P("col", "row"))
    return jax.shard_map(
        body,
        mesh=mesh,
        in_specs=placed,
        out_specs=(P("row", "col"), P("col", "row")),
        check_vma=False,
    )
```

profile of v0, /device:TPU:32, one launch (start us, length us, event | category | flops | bytes accessed | tf_op | source)
XLA Modules:
  0.0 351.7 jit_solution(12061191900237767093)
XLA Ops:
  7.2 0.0 all-gather.3.cloned.1.call-start
  7.2 0.7 all-gather.3.cloned.1.call-update
  7.9 0.0 all-reduce.2.cloned.1.call-start
  8.0 84.9 %all-gather.3.cloned.1.call-done = bf16[8192,512]{1,0:T(8,128)(2,1)} async-done(((bf16[256,512]{1,0:T(8,128)(2,1)}), bf16[8192,512]{1,0:T(8,128)(2,1)}) %all-gather.3.cloned.1.call-update) | async-done | bytes 8388624 | tf_op jit(solution)/shard_map/all_gather | solution.py:29
  92.8 4.9 %dynamic-slice_select_fusion = bf16[8192,256]{1,0:T(8,128)(2,1)} fusion(bf16[8192,512]{1,0:T(8,128)(2,1)} %all-gather.3.cloned.1.call-done, s32[]{:T(128)S(6)} %select_n.38, pred[]{:T(512)S(6)} %eq.18), kind=kLoop, calls=%fused_computation | loop fusion | flops 2097152 | bytes 8388613 | tf_op jit(solution)/shard_map/jit(_where)/select_n | solution.py:10
  97.7 0.0 all-reduce.2.cloned.1.call-update
  97.7 0.0 all-gather.5.cloned.1.call-start
  97.8 0.7 all-gather.5.cloned.1.call-update
  98.5 130.4 %all-reduce.2.cloned.1.call-done = bf16[8192,256]{1,0:T(8,128)(2,1)} async-done(((bf16[8192,256]{1,0:T(8,128)(2,1)}), bf16[8192,256]{1,0:T(8,128)(2,1)}) %all-reduce.2.cloned.1.call-update) | async-done | bytes 4194320 | tf_op jit(solution)/shard_map/psum | solution.py:11
  228.9 7.0 %fusion.1 = f32[256,512]{1,0:T(8,128)S(1)} fusion(bf16[8192,256]{1,0:T(8,128)(2,1)} %all-reduce.2.cloned.1.call-done, bf16[8192,512]{1,0:T(8,128)(2,1)} %all-gather.3.cloned.1.call-done), kind=kOutput, calls=%fused_computation.10 | convolution fusion | flops 2147483648 | bytes 13107200 | tf_op jit(solution)/shard_map/dot_general | solution.py:34
  235.9 0.0 copy-start
  235.9 66.4 %all-gather.5.cloned.1.call-done = bf16[512,2048]{0,1:T(8,128)(2,1)} async-done(((bf16[512,64]{0,1:T(8,128)(2,1)}), bf16[512,2048]{0,1:T(8,128)(2,1)}) %all-gather.5.cloned.1.call-update) | async-done | bytes 2097168 | tf_op jit(solution)/shard_map/all_gather | solution.py:37
  302.3 2.3 convolution_bitcast_fusion
  304.7 0.0 copy-start.1
  304.7 1.5 copy.14
  306.2 0.0 copy-done
  306.2 6.9 %all-to-all-start = ((f32[16,128,256]{1,2,0:T(8,128)}), f32[16,128,256]{1,2,0:T(8,128)S(1)}, u32[]{:S(2)}, u32[]{:S(2)}) async-start(f32[16,128,256]{1,2,0:T(8,128)} %bitcast.9), calls=%async_computation | async-start | bytes 4194304 | tf_op jit(solution)/shard_map/all_to_all | solution.py:22
  313.1 0.0 copy-done.1
  313.1 0.1 compare_reduce_fusion
  313.2 30.9 %all-to-all-done = f32[16,128,256]{1,2,0:T(8,128)S(1)} async-done(((f32[16,128,256]{1,2,0:T(8,128)}), f32[16,128,256]{1,2,0:T(8,128)S(1)}, u32[]{:S(2)}, u32[]{:S(2)}) %all-to-all-start) | async-done | bytes 2097184 | tf_op jit(solution)/shard_map/all_to_all | solution.py:22
  344.2 0.1 reduce_sum.9
  344.3 0.1 negate_select_fusion
  344.4 0.8 copy.10
  (1 shorter events, 0.0 us)
Async XLA Ops:
  7.2 85.7 %all-gather.3.cloned.1.call-start = ((), (), s32[]{:S(2)}) async-start(), calls=%async_computation.1 | async-start | bytes 8650752 | tf_op jit(solution)/shard_map/all_gather | solution.py:29
  7.9 221.0 %all-reduce.2.cloned.1.call-start = ((), (), s32[]{:S(2)}) async-start(), calls=%async_computation.2 | async-start | bytes 8388608 | tf_op jit(solution)/shard_map/psum | solution.py:11
  97.7 204.6 %all-gather.5.cloned.1.call-start = ((), (), s32[]{:S(2)}) async-start(), calls=%async_computation.3 | async-start | bytes 2162688 | tf_op jit(solution)/shard_map/all_gather | solution.py:37
  235.9 70.3 %copy-start = (f32[256,512]{1,0:T(8,128)}, f32[256,512]{1,0:T(8,128)S(1)}, u32[]{:S(2)}) copy-start(f32[256,512]{1,0:T(8,128)S(1)} %fusion.1) | copy-start | bytes 1572868
  304.7 8.5 %copy-start.1 = (s32[32]{0:T(128)S(1)}, s32[32]{0:T(128)}, u32[]{:S(2)}) copy-start(s32[32]{0:T(128)} %param.4) | copy-start | bytes 388
  306.2 37.9 %all-to-all-start = ((f32[16,128,256]{1,2,0:T(8,128)}), f32[16,128,256]{1,2,0:T(8,128)S(1)}, u32[]{:S(2)}, u32[]{:S(2)}) async-start(f32[16,128,256]{1,2,0:T(8,128)} %bitcast.9), calls=%async_computation | async-start | bytes 4194304 | tf_op jit(solution)/shard_map/all_to_all | solution.py:22
Sparse Core Ops, SparseCore 0:
  10.1 82.6 all-gather.2
  97.8 130.9 all-reduce.1
  231.0 71.2 all-gather.4
where the time goes:
time: 352 us
  waiting for transfers between devices  314 us (89%)
  between operations  13.8 us (4%)
  matrix products  9.32 us (3%)
  starting transfers between devices  7.01 us (2%)
  other arithmetic  5.17 us (1%)
    psum x1, waiting for transfers between devices, from_root(): return lax.psum(kept, axis)  130 us
    all_gather x1, waiting for transfers between devices, body(): whole = lax.all_gather(factor, 'row', axis=0, tiled=True)  84.9 us
    all_gather x1, waiting for transfers between devices, body(): coupling_full = lax.all_gather(coupling, 'row', axis=1, tiled=True)  66.4 us
    all_to_all x1, waiting for transfers between devices, summed_on_arrival(): lax.all_to_all(in_blocks(value, dim, devices), axis, 0, 0, tiled=True)  30.9 us
  transfers between devices with their start and end apart: 4, of which 4 were waited for; matrix products, arithmetic and copies ran while one was open for 2% of the time, Pallas kernels for 0%

commit v1 on v0

--- a/solution.py
+++ b/solution.py
@@ -26,7 +26,15 @@
 def body(factor, sel_tiles, coupling):
     rows_here = factor.shape[0]
     row_index = lax.axis_index("row")
-    whole = lax.all_gather(factor, "row", axis=0, tiled=True)
+    whole = jnp.concatenate(
+        lax.all_to_all(
+            jnp.stack([factor] * lax.axis_size("row"), axis=0),
+            axis_name="row",
+            split_axis=0,
+            concat_axis=0,
+        ),
+        axis=0,
+    )
     ratio = lax.axis_size("row") // lax.axis_size("col")
     offset = row_index % ratio * rows_here
     piece = lax.dynamic_slice_in_dim(whole, offset, rows_here, 1)

time: 352 us -> 585 us (1.66)
  waiting for transfers between devices: 314 us -> 526 us
  starting transfers between devices: 7.01 us -> 20.8 us
    all_to_all x0 -> x1, waiting for transfers between devices: none -> 370 us  [body(): lax.all_to_all(jnp.stack([factor] * lax.axis_size('row'), axis=0), axis_n...]
    all_gather x1 -> x0, waiting for transfers between devices: 84.9 us -> none  [body(): whole = lax.all_gather(factor, 'row', axis=0, tiled=True)]
    all_gather x1, waiting for transfers between devices: 66.4 us -> 0.03 us  [body(): coupling_full = lax.all_gather(coupling, 'row', axis=1, tiled=True)]
    all_to_all x0 -> x1, starting transfers between devices: none -> 15.4 us  [body(): lax.all_to_all(jnp.stack([factor] * lax.axis_size('row'), axis=0), axis_n...]
  transfers between devices with their start and end apart: 4 -> 4, of which waited for: 4 -> 3; matrix products, arithmetic and copies ran while one was open for 2% -> 1% of each run, Pallas kernels for 0% -> 0%
where the time goes in v1:
time: 585 us
  waiting for transfers between devices  526 us (90%)
  starting transfers between devices  20.8 us (4%)
  between operations  15.6 us (3%)
  matrix products  9.48 us (2%)
  local copies, waits for them, and re-layouts  7.43 us (1%)
    all_to_all x1, waiting for transfers between devices, body(): lax.all_to_all(jnp.stack([factor] * lax.axis_size('row'), axis=0), axis_n...  370 us
    psum x1, waiting for transfers between devices, from_root(): return lax.psum(kept, axis)  126 us
    all_to_all x1, waiting for transfers between devices, summed_on_arrival(): lax.all_to_all(in_blocks(value, dim, devices), axis, 0, 0, tiled=True)  30 us
    all_to_all x1, starting transfers between devices, body(): lax.all_to_all(jnp.stack([factor] * lax.axis_size('row'), axis=0), axis_n...  15.4 us
  transfers between devices with their start and end apart: 4, of which 3 were waited for; matrix products, arithmetic and copies ran while one was open for 1% of the time, Pallas kernels for 0%

profile of v1, /device:TPU:32, one launch (start us, length us, event | category | flops | bytes accessed | tf_op | source)
XLA Modules:
  0.0 584.9 jit_solution(17080301382215973626)
XLA Ops:
  8.0 5.1 stack.2
  13.1 15.4 %all-to-all-start = ((bf16[32,256,512]{2,1,0:T(8,128)(2,1)}), bf16[32,256,512]{2,1,0:T(8,128)(2,1)}, u32[]{:S(2)}, u32[]{:S(2)}) async-start(bf16[32,256,512]{2,1,0:T(8,128)(2,1)} %stack.2), calls=%async_computation | async-start | bytes 16777216 | tf_op jit(solution)/shard_map/all_to_all | solution.py:30
  28.5 0.0 all-reduce.2.cloned.1.call-start
  28.6 369.9 %all-to-all-done = bf16[32,256,512]{2,1,0:T(8,128)(2,1)} async-done(((bf16[32,256,512]{2,1,0:T(8,128)(2,1)}), bf16[32,256,512]{2,1,0:T(8,128)(2,1)}, u32[]{:S(2)}, u32[]{:S(2)}) %all-to-all-start) | async-done | bytes 8388640 | tf_op jit(solution)/shard_map/all_to_all | solution.py:30
  398.5 4.9 dynamic-slice_select_fusion
  403.3 0.0 all-reduce.2.cloned.1.call-update
  403.3 0.0 all-gather.2.cloned.1.call-start
  403.4 0.5 all-gather.2.cloned.1.call-update
  403.9 126.1 %all-reduce.2.cloned.1.call-done = bf16[8192,256]{1,0:T(8,128)(2,1)} async-done(((bf16[8192,256]{1,0:T(8,128)(2,1)}), bf16[8192,256]{1,0:T(8,128)(2,1)}) %all-reduce.2.cloned.1.call-update) | async-done | bytes 4194320 | tf_op jit(solution)/shard_map/psum | solution.py:11
  530.0 7.0 %fusion.1 = f32[256,512]{1,0:T(8,128)S(1)} fusion(bf16[8192,256]{1,0:T(8,128)(2,1)} %all-reduce.2.cloned.1.call-done, bf16[8192,512]{1,0:T(8,128)(2,1)} %bitcast), kind=kOutput, calls=%fused_computation.10 | convolution fusion | flops 2147483648 | bytes 13107200 | tf_op jit(solution)/shard_map/dot_general | solution.py:42
  537.0 0.0 copy-start
  537.0 0.0 all-gather.2.cloned.1.call-done
  537.0 2.5 convolution_bitcast_fusion
  539.5 0.0 copy-start.1
  539.6 1.5 copy.14
  541.1 0.0 copy-done
  541.1 5.3 all-to-all-start.1
  546.5 0.0 copy-done.1
  546.5 0.1 compare_reduce_fusion
  546.6 30.0 %all-to-all-done.1 = f32[16,128,256]{1,2,0:T(8,128)S(1)} async-done(((f32[16,128,256]{1,2,0:T(8,128)}), f32[16,128,256]{1,2,0:T(8,128)S(1)}, u32[]{:S(2)}, u32[]{:S(2)}) %all-to-all-start.1) | async-done | bytes 2097184 | tf_op jit(solution)/shard_map/all_to_all | solution.py:22
  576.5 0.1 reduce_sum.9
  576.6 0.1 negate_select_fusion
  576.7 0.8 copy.10
  (1 shorter events, 0.0 us)
Async XLA Ops:
  13.1 385.3 %all-to-all-start = ((bf16[32,256,512]{2,1,0:T(8,128)(2,1)}), bf16[32,256,512]{2,1,0:T(8,128)(2,1)}, u32[]{:S(2)}, u32[]{:S(2)}) async-start(bf16[32,256,512]{2,1,0:T(8,128)(2,1)} %stack.2), calls=%async_computation | async-start | bytes 16777216 | tf_op jit(solution)/shard_map/all_to_all | solution.py:30
  28.5 501.5 %all-reduce.2.cloned.1.call-start = ((), (), s32[]{:S(2)}) async-start(), calls=%async_computation.2 | async-start | bytes 8388608 | tf_op jit(solution)/shard_map/psum | solution.py:11
  403.3 133.7 %all-gather.2.cloned.1.call-start = ((), (), s32[]{:S(2)}) async-start(), calls=%async_computation.3 | async-start | bytes 2162688 | tf_op jit(solution)/shard_map/all_gather | solution.py:45
  537.0 4.1 copy-start
  539.5 6.9 %copy-start.1 = (s32[32]{0:T(128)S(1)}, s32[32]{0:T(128)}, u32[]{:S(2)}) copy-start(s32[32]{0:T(128)} %param.4) | copy-start | bytes 388
  541.1 35.4 %all-to-all-start.1 = ((f32[16,128,256]{1,2,0:T(8,128)}), f32[16,128,256]{1,2,0:T(8,128)S(1)}, u32[]{:S(2)}, u32[]{:S(2)}) async-start(f32[16,128,256]{1,2,0:T(8,128)} %bitcast.10), calls=%async_computation.1 | async-start | bytes 4194304 | tf_op jit(solution)/shard_map/all_to_all | solution.py:22
Sparse Core Ops, SparseCore 0:
  403.5 126.4 all-reduce.1
Sparse Core Ops, SparseCore 1:
  406.0 63.6 all-gather.1
